TPU v7x, 32 devices: a whole 2x2x4 slice. The times are simulated.
32 devices in a mesh: task: 4 (over z), mp: 8 (over y, x, core).
Axes of the slice: x: 2, y: 2, z: 4, core: 2. Of those that a mesh axis runs over, the one named last changes fastest.
Arguments:
- deter: float32 [1024, 4096], P('task', 'mp'), may hold values from -3 to 3
- draws: int32 [4, 32, 1024], P(None, None, 'task'), may hold values from 0 to 31
- actions: int32 [4, 1024], P(None, 'task'), may hold values from 0 to 17
- horizons: int32 [64], replicated, may hold values from 5 to 30, as said below
- offsets: int32 [4, 4], replicated, may hold values from 0 to 3, as said below
- embed_stoch: bfloat16 [1024, 1024], replicated, may hold values from -1 to 1
- embed_act: bfloat16 [18, 1024], replicated, may hold values from -6 to 6
- gru_weight: bfloat16 [5120, 3, 4096], P(None, None, 'mp'), may hold values from -0.078125 to 0.078125
- prior_weight: bfloat16 [4096, 1024], replicated, may hold values from -0.09375 to 0.09375
- logit_weight: bfloat16 [1024, 1024], replicated, may hold values from -0.75 to 0.75
- head_weight: bfloat16 [1024, 2], replicated, may hold values from -0.375 to 0.375
Outputs:
- log_prob: float32 [4, 1024], P(None, 'task')
- reward: float32 [4, 1024], P(None, 'task')
- continuation: float32 [4, 1024], P(None, 'task')
- final_deter: float32 [1024, 4096], P('task', 'mp')
Inputs may be any that keep to these rules, and one draw needn't show every extreme that they name: `horizons`: rows of task k are home rows k * (16) up to (k + 1) * 16 - 1. `offsets`: the 4 numbers of one row are distinct.
All inputs are finite; a program needn't handle non-finite values.
Results may differ from a plain program's by a relative error of at most 0.0045.
Values may be sent and summed in bfloat16 or wider, within the bound.
A program may use at most 128 MiB of HBM per device.

v0:
```python
import jax
import jax.numpy as jnp
from jax import lax
from jax.sharding import PartitionSpec as P

HID = 1024
GROUPS = 32
CLASSES = 32
ACTS = 18
TASKS = 64
BLK_DEV = 4
STEPS = 4
WSTART = 16


def normed_rows(values):
    entries = values.shape[-1]
    average = jnp.sum(values, axis=-1, keepdims=True) / entries
    squares = jnp.sum(values * values, axis=-1, keepdims=True) / entries
    return (values - average) * lax.rsqrt(squares - average * average + 1e-05)


def product(rows_in, weight):
    return jnp.dot(rows_in, weight, preferred_element_type=jnp.float32)


def recurrence(deter, embedded, gate_weight, living, det_full):
    carried = deter
    rows_here, det_share = deter.shape
    lows = []
    for moment in range(STEPS):
        low = carried.astype(jnp.bfloat16)
        gathered = lax.all_gather(low, "mp", axis=1, tiled=True)
        lows.append(gathered)
        joined = jnp.concatenate([embedded[moment], gathered], axis=1)
        parts = [product(joined, gate_weight[part]) for part in range(3)]
        sums = sum((jnp.sum(part, axis=1) for part in parts))
        squares = sum((jnp.sum(part * part, axis=1) for part in parts))
        sums, squares = lax.psum(jnp.stack([sums, squares]), "mp")
        average = sums / (3 * det_full)
        inverse = lax.rsqrt(squares / (3 * det_full) - average * average + 1e-05)
        normed = [(part - average[:, None]) * inverse[:, None] for part in parts]
        reset_gate = jax.nn.sigmoid(normed[0])
        candidate = jnp.tanh(reset_gate * normed[1])
        update = jax.nn.sigmoid(normed[2] - 1.0)
        renewed = update * candidate + (1.0 - update) * carried
        carried = jnp.where(living[moment][:, None] > 0, renewed, carried)
    return (carried, lows)


def on_device(
    deter,
    draws,
    actions,
    horizons,
    offsets,
    embed_stoch,
    embed_act,
    gru_weight,
    prior_weight,
    logit_weight,
    head_weight,
):
    holders = lax.axis_size("task")
    device = lax.axis_index("task")
    shards = lax.axis_size("mp")
    shard_index = lax.axis_index("mp")
    rows_here, det_share = deter.shape
    block_rows = rows_here // BLK_DEV
    per_task = rows_here * holders // TASKS
    own_rows = rows_here // shards
    places = jnp.arange(holders, dtype=jnp.int32)
    classes = jnp.arange(CLASSES, dtype=jnp.int32)
    running = jnp.cumsum(offsets, axis=0) % holders
    packed = jnp.concatenate([draws, actions[:, None]], axis=1).astype(jnp.bfloat16)
    packed = lax.all_gather(packed, "task")
    packed = packed.reshape(holders, STEPS, GROUPS + 1, BLK_DEV, block_rows)
    at_slot = (device + running) % holders
    picked = places[:, None, None] == at_slot[None]
    packed = jnp.sum(
        jnp.where(picked[:, :, None, :, None], packed.astype(jnp.float32), 0.0), axis=0
    ).astype(jnp.int32)
    packed = packed.reshape(STEPS, GROUPS + 1, rows_here)
    draws_home = jnp.transpose(packed[:, :GROUPS], (0, 2, 1))
    hot = (draws_home[:, :, :, None] == classes).astype(jnp.bfloat16)
    hot = hot.reshape(STEPS * rows_here, GROUPS * CLASSES)
    action_hot = (
        packed[:, GROUPS].reshape(-1)[:, None] == jnp.arange(ACTS, dtype=jnp.int32)
    ).astype(jnp.bfloat16)
    embed_pre = product(hot, embed_stoch) + product(action_hot, embed_act)
    embedded = jax.nn.silu(normed_rows(embed_pre)).astype(jnp.bfloat16)
    embedded = embedded.reshape(STEPS, rows_here, HID)
    home_rows = device * rows_here + jnp.arange(rows_here, dtype=jnp.int32)
    task_ids = jnp.arange(TASKS, dtype=jnp.int32)
    horizon_rows = jnp.sum(
        jnp.where((home_rows // per_task)[:, None] == task_ids, horizons, 0), axis=1
    )
    alive = horizon_rows[None] > WSTART + jnp.arange(STEPS, dtype=jnp.int32)[:, None]
    living = alive.astype(jnp.float32)
    gate_weight = jnp.transpose(gru_weight, (1, 0, 2))
    carried, lows = recurrence(deter, embedded, gate_weight, living, det_share * shards)
    target = (device + running[-1]) % holders
    sending = places[:, None] == target[None, :]
    blocks = carried.reshape(BLK_DEV, block_rows, det_share)
    outgoing = jnp.where(sending[:, :, None, None], blocks[None], 0.0).astype(jnp.bfloat16)
    arrived = lax.all_to_all(
        outgoing.reshape(holders * BLK_DEV * block_rows, det_share),
        "task",
        split_axis=0,
        concat_axis=0,
        tiled=True,
    ).reshape(holders, BLK_DEV, block_rows, det_share)
    taking = places[:, None] == ((device - running[-1]) % holders)[None, :]
    final = jnp.sum(
        jnp.where(taking[:, :, None, None], arrived.astype(jnp.float32), 0.0), axis=0
    ).reshape(rows_here, det_share)

    def own(array, axis):
        return lax.dynamic_slice_in_dim(array, shard_index * own_rows, own_rows, axis)

    state_rows = jnp.concatenate([own(low, 0) for low in lows], axis=0)
    hidden = jax.nn.silu(normed_rows(product(state_rows, prior_weight))).astype(jnp.bfloat16)
    raw = product(hidden, logit_weight).reshape(STEPS * own_rows, GROUPS, CLASSES)
    exponent = jnp.exp(5.0 * jnp.tanh(raw / 5.0))
    own_hot = own(draws_home, 1).reshape(STEPS * own_rows, GROUPS)[:, :, None] == classes
    chosen = jnp.sum(jnp.where(own_hot, exponent, 0.0), axis=-1)
    chances = 0.99 * chosen / jnp.sum(exponent, axis=-1) + 0.01 / CLASSES
    log_prob = jnp.sum(jnp.log(chances), axis=-1)
    head_out = product(hidden, head_weight)
    results = jnp.stack([log_prob, head_out[:, 0], jax.nn.sigmoid(head_out[:, 1])])
    results = results.reshape(3, STEPS, own_rows) * own(living, 1)[None]
    spread = lax.all_gather(results, ("task", "mp"))
    spread = spread.reshape(holders, shards, 3, STEPS, own_rows)
    spread = jnp.transpose(spread, (0, 2, 3, 1, 4)).reshape(holders, 3, STEPS, BLK_DEV, block_rows)
    source = (device - running) % holders
    from_home = places[:, None, None] == source[None]
    outs = jnp.sum(jnp.where(from_home[:, None, :, :, None], spread, 0.0), axis=0)
    outs = outs.reshape(3, STEPS, rows_here)
    return (outs[0], outs[1], outs[2], final)


def solution(mesh):
    in_specs = (
        P("task", "mp"),
        P(None, None, "task"),
        P(None, "task"),
        P(),
        P(),
        P(),
        P(),
        P(None, None, "mp"),
        P(),
        P(),
        P(),
    )
    out_specs = (P(None, "task"), P(None, "task"), P(None, "task"), P("task", "mp"))
    return jax.shard_map(
        on_device, mesh=mesh, in_specs=in_specs, out_specs=out_specs, check_vma=False
    )
```

profile of v0, /device:TPU:0, one launch (start us, length us, event | category | flops | bytes accessed | tf_op | source)
XLA Modules:
  0.0 310.5 jit_solution(17363063580489032251)
XLA Ops:
  7.2 1.9 convert_element_type.50
  9.2 0.7 convert_bitcast_fusion
  9.9 0.7 reduce_window_sum.11
  10.8 0.1 broadcast_in_dim.159
  11.0 0.9 convert.10
  12.0 15.7 %all_gather.20 = bf16[4,4,33,256]{3,1,2,0:T(4,128)(2,1)S(1)} all-gather(bf16[1,4,33,256]{3,1,2,0:T(4,128)(2,1)S(1)} %pad_maximum_fusion.16), channel_id=1, replica_groups=mesh['task'=4,'mp'=8] {'task'}, dimensions={0}, use_global_device_ids=true | all-gather | bytes 337920 | tf_op jit(solution)/shard_map/all_gather | solution.py:76
  27.7 0.2 select_reduce_fusion.1
  27.9 0.1 copy.59
  28.0 0.5 eq.155
  28.6 1.0 copy.69
  29.6 2.6 fusion
  32.2 1.5 fusion.47
  33.7 1.4 multiply_convert_fusion
  35.1 0.9 fusion.64
  36.0 0.2 copy.60
  36.3 0.1 select_reduce_fusion.4
  36.5 4.2 %all-gather.5.cloned.1.call-done = bf16[256,4096]{1,0:T(8,128)(2,1)} async-done(((bf16[256,512]{1,0:T(8,128)(2,1)}), bf16[256,4096]{1,0:T(8,128)(2,1)}) %all-gather.5.cloned.1.call-update) | async-done | bytes 2097168 | tf_op jit(solution)/shard_map/all_gather | solution.py:33
  40.7 4.9 %fusion.59 = (f32[256]{0:T(256)S(1)}, f32[256]{0:T(256)S(1)}, f32[256,512]{1,0:T(8,128)S(1)}) fusion(bf16[3,5120,512]{2,1,0:T(8,128)(2,1)} %bitcast.126, bf16[256,4096]{1,0:T(8,128)(2,1)} %all-gather.5.cloned.1.call-done, bf16[256,1024]{1,0:T(8,128)(2,1)S(1)} %copy.60), kind=kOutput, calls=%fused_computation.170 | convolution fusion | flops 1347812864 | bytes 8390656 | tf_op jit(solution)/shard_map/dot_general | solution.py:24
  45.6 4.8 %fusion.58 = (f32[256]{0:T(256)S(1)}, f32[256]{0:T(256)S(1)}, f32[256,512]{1,0:T(8,128)}) fusion(bf16[3,5120,512]{2,1,0:T(8,128)(2,1)} %bitcast.127, bf16[256,4096]{1,0:T(8,128)(2,1)S(1)} %copy-done.5, bf16[256,1024]{1,0:T(8,128)(2,1)S(1)} %copy.60), kind=kOutput, calls=%fused_computation.169 | convolution fusion | flops 1347812864 | bytes 8390656 | tf_op jit(solution)/shard_map/dot_general | solution.py:24
  50.4 4.9 %fusion.60 = (f32[256]{0:T(256)S(1)}, f32[256]{0:T(256)S(1)}, f32[256,512]{1,0:T(8,128)}) fusion(bf16[3,5120,512]{2,1,0:T(8,128)(2,1)} %bitcast.128, bf16[256,4096]{1,0:T(8,128)(2,1)S(1)} %copy-done.5, bf16[256,1024]{1,0:T(8,128)(2,1)S(1)} %copy.60), kind=kOutput, calls=%fused_computation.171 | convolution fusion | flops 1347812864 | bytes 8390656 | tf_op jit(solution)/shard_map/dot_general | solution.py:24
  55.4 13.1 %psum.28 = f32[2,256]{1,0:T(2,128)S(1)} all-reduce(f32[2,256]{1,0:T(2,128)S(1)} %pad_maximum_fusion.17), channel_id=1, replica_groups=mesh['task'=4,'mp'=8] {'mp'}, use_global_device_ids=true, to_apply=%region_11.12 | all-reduce | flops 512 | bytes 4096 | tf_op jit(solution)/shard_map/psum | solution.py:39
  68.5 2.4 fusion.63
  70.9 0.2 all-gather.9.cloned.1.call-start
  71.1 0.2 copy.61
  71.3 27.8 %all-gather.7.cloned.1.call-done = bf16[256,4096]{1,0:T(8,128)(2,1)} async-done(((bf16[256,512]{1,0:T(8,128)(2,1)}), bf16[256,4096]{1,0:T(8,128)(2,1)}) %all-gather.7.cloned.1.call-update) | async-done | bytes 2097168 | tf_op jit(solution)/shard_map/all_gather | solution.py:33
  99.1 4.9 %fusion.56 = (f32[256]{0:T(256)S(1)}, f32[256]{0:T(256)S(1)}, f32[256,512]{1,0:T(8,128)S(1)}) fusion(bf16[3,5120,512]{2,1,0:T(8,128)(2,1)} %bitcast.129, bf16[256,4096]{1,0:T(8,128)(2,1)} %all-gather.7.cloned.1.call-done, bf16[256,1024]{1,0:T(8,128)(2,1)S(1)} %copy.61), kind=kOutput, calls=%fused_computation.167 | convolution fusion | flops 1347812864 | bytes 8390656 | tf_op jit(solution)/shard_map/dot_general | solution.py:24
  104.0 4.8 %fusion.55 = (f32[256]{0:T(256)S(1)}, f32[256]{0:T(256)S(1)}, f32[256,512]{1,0:T(8,128)}) fusion(bf16[3,5120,512]{2,1,0:T(8,128)(2,1)} %bitcast.130, bf16[256,4096]{1,0:T(8,128)(2,1)S(1)} %copy-done.6, bf16[256,1024]{1,0:T(8,128)(2,1)S(1)} %copy.61), kind=kOutput, calls=%fused_computation.166 | convolution fusion | flops 1347812864 | bytes 8390656 | tf_op jit(solution)/shard_map/dot_general | solution.py:24
  108.8 4.8 %fusion.57 = (f32[256]{0:T(256)S(1)}, f32[256]{0:T(256)S(1)}, f32[256,512]{1,0:T(8,128)}) fusion(bf16[3,5120,512]{2,1,0:T(8,128)(2,1)} %bitcast.131, bf16[256,4096]{1,0:T(8,128)(2,1)S(1)} %copy-done.6, bf16[256,1024]{1,0:T(8,128)(2,1)S(1)} %copy.61), kind=kOutput, calls=%fused_computation.168 | convolution fusion | flops 1347812864 | bytes 8390656 | tf_op jit(solution)/shard_map/dot_general | solution.py:24
  113.7 13.1 %psum.29 = f32[2,256]{1,0:T(2,128)S(1)} all-reduce(f32[2,256]{1,0:T(2,128)S(1)} %pad_maximum_fusion.18), channel_id=1, replica_groups=mesh['task'=4,'mp'=8] {'mp'}, use_global_device_ids=true, to_apply=%region_18.19 | all-reduce | flops 512 | bytes 4096 | tf_op jit(solution)/shard_map/psum | solution.py:39
  126.8 2.4 fusion.62
  129.2 0.2 copy.62
  129.4 28.0 %all-gather.9.cloned.1.call-done = bf16[256,4096]{1,0:T(8,128)(2,1)} async-done(((bf16[256,512]{1,0:T(8,128)(2,1)}), bf16[256,4096]{1,0:T(8,128)(2,1)}) %all-gather.9.cloned.1.call-update) | async-done | bytes 2097168 | tf_op jit(solution)/shard_map/all_gather | solution.py:33
  157.4 4.9 %fusion.53 = (f32[256]{0:T(256)S(1)}, f32[256]{0:T(256)S(1)}, f32[256,512]{1,0:T(8,128)S(1)}) fusion(bf16[3,5120,512]{2,1,0:T(8,128)(2,1)} %bitcast.132, bf16[256,4096]{1,0:T(8,128)(2,1)} %all-gather.9.cloned.1.call-done, bf16[256,1024]{1,0:T(8,128)(2,1)S(1)} %copy.62), kind=kOutput, calls=%fused_computation.164 | convolution fusion | flops 1347812864 | bytes 8390656 | tf_op jit(solution)/shard_map/dot_general | solution.py:24
  162.4 4.1 %fusion.52 = (f32[256]{0:T(256)S(1)}, f32[256]{0:T(256)S(1)}, f32[256,512]{1,0:T(8,128)S(1)}) fusion(bf16[3,5120,512]{2,1,0:T(8,128)(2,1)} %bitcast.133, bf16[256,4096]{1,0:T(8,128)(2,1)S(1)} %copy-done.7, bf16[256,1024]{1,0:T(8,128)(2,1)S(1)} %copy.62), kind=kOutput, calls=%fused_computation.163 | convolution fusion | flops 1347812864 | bytes 8390656 | tf_op jit(solution)/shard_map/dot_general | solution.py:24
  166.5 4.8 %fusion.54 = (f32[256]{0:T(256)S(1)}, f32[256]{0:T(256)S(1)}, f32[256,512]{1,0:T(8,128)}) fusion(bf16[3,5120,512]{2,1,0:T(8,128)(2,1)} %bitcast.134, bf16[256,4096]{1,0:T(8,128)(2,1)S(1)} %copy-done.7, bf16[256,1024]{1,0:T(8,128)(2,1)S(1)} %copy.62), kind=kOutput, calls=%fused_computation.165 | convolution fusion | flops 1347812864 | bytes 8390656 | tf_op jit(solution)/shard_map/dot_general | solution.py:24
  171.3 13.1 %psum.30 = f32[2,256]{1,0:T(2,128)S(1)} all-reduce(f32[2,256]{1,0:T(2,128)S(1)} %pad_maximum_fusion.19), channel_id=1, replica_groups=mesh['task'=4,'mp'=8] {'mp'}, use_global_device_ids=true, to_apply=%region_25.26 | all-reduce | flops 512 | bytes 4096 | tf_op jit(solution)/shard_map/psum | solution.py:39
  184.4 2.2 fusion.61
  186.7 0.1 copy.54
  187.3 0.1 eq.148
  187.4 0.2 copy.67
  187.7 1.0 constant_dynamic-slice_fusion.4
  188.7 1.7 constant_dynamic-slice_fusion.3
  190.3 1.7 constant_dynamic-slice_fusion.2
  192.0 22.9 %all-gather.11.cloned.1.call-done = bf16[256,4096]{1,0:T(8,128)(2,1)} async-done(((bf16[256,512]{1,0:T(8,128)(2,1)}), bf16[256,4096]{1,0:T(8,128)(2,1)}) %all-gather.11.cloned.1.call-update) | async-done | bytes 2097168 | tf_op jit(solution)/shard_map/all_gather | solution.py:33
  214.9 4.9 %fusion.49 = (f32[256]{0:T(256)S(1)}, f32[256]{0:T(256)S(1)}, f32[256,512]{1,0:T(8,128)S(1)}) fusion(bf16[3,5120,512]{2,1,0:T(8,128)(2,1)} %bitcast.135, bf16[256,4096]{1,0:T(8,128)(2,1)} %all-gather.11.cloned.1.call-done, bf16[256,1024]{1,0:T(8,128)(2,1)S(1)} %copy.67), kind=kOutput, calls=%fused_computation.160 | convolution fusion | flops 1347812864 | bytes 8390656 | tf_op jit(solution)/shard_map/dot_general | solution.py:24
  219.8 4.1 %fusion.48 = (f32[256]{0:T(256)S(1)}, f32[256]{0:T(256)S(1)}, f32[256,512]{1,0:T(8,128)S(1)}) fusion(bf16[3,5120,512]{2,1,0:T(8,128)(2,1)} %bitcast.136, bf16[256,4096]{1,0:T(8,128)(2,1)S(1)} %copy-done.8, bf16[256,1024]{1,0:T(8,128)(2,1)S(1)} %copy.67), kind=kOutput, calls=%fused_computation.159 | convolution fusion | flops 1347812864 | bytes 8390656 | tf_op jit(solution)/shard_map/dot_general | solution.py:24
  224.0 4.1 %fusion.50 = (f32[256]{0:T(256)S(1)}, f32[256]{0:T(256)S(1)}, f32[256,512]{1,0:T(8,128)S(1)}) fusion(bf16[3,5120,512]{2,1,0:T(8,128)(2,1)} %bitcast.137, bf16[256,4096]{1,0:T(8,128)(2,1)S(1)} %copy-done.8, bf16[256,1024]{1,0:T(8,128)(2,1)S(1)} %copy.67), kind=kOutput, calls=%fused_computation.161 | convolution fusion | flops 1347812864 | bytes 8390656 | tf_op jit(solution)/shard_map/dot_general | solution.py:24
  228.1 13.3 %psum.31 = f32[2,256]{1,0:T(2,128)S(1)} all-reduce(f32[2,256]{1,0:T(2,128)S(1)} %pad_maximum_fusion.20), channel_id=1, replica_groups=mesh['task'=4,'mp'=8] {'mp'}, use_global_device_ids=true, to_apply=%region_38.39 | all-reduce | flops 512 | bytes 4096 | tf_op jit(solution)/shard_map/psum | solution.py:39
  241.5 0.5 add_select_fusion
  241.9 1.2 select_convert_fusion
  243.1 4.6 %all-to-all-start = ((bf16[4,256,512]{2,1,0:T(8,128)(2,1)}), bf16[4,256,512]{2,1,0:T(8,128)(2,1)S(1)}, u32[]{:S(2)}, u32[]{:S(2)}) async-start(bf16[4,256,512]{2,1,0:T(8,128)(2,1)} %select_convert_fusion), calls=%async_computation | async-start | bytes 2097152 | tf_op jit(solution)/shard_map/all_to_all | solution.py:106
  247.7 1.0 constant_dynamic-slice_fusion.1
  248.7 5.1 %fusion.51 = (f32[128]{0:T(128)S(1)}, f32[128]{0:T(128)S(1)}, f32[128,1024]{1,0:T(8,128)S(1)}) fusion(bf16[4096,1024]{1,0:T(8,128)(2,1)} %param.19, bf16[32,4096]{1,0:T(8,128)(2,1)S(1)} %constant_dynamic-slice_fusion.1, bf16[32,4096]{1,0:T(8,128)(2,1)} %constant_dynamic-slice_fusion.2, bf16[32,4096]{1,0:T(8,128)(2,1)} %constant_dynamic-slice_fusion.3, ...), kind=kOutput, calls=%fused_computation.162 | convolution fusion | flops 1078329088 | bytes 9962496 | tf_op jit(solution)/shard_map/dot_general | solution.py:24
  253.8 0.3 multiply_convert_fusion.1
  254.1 0.2 fusion.67
  254.5 2.9 fusion.17
  257.3 2.1 copy.63
  259.4 1.3 select_reduce_fusion.2
  260.8 40.0 %all_gather.25 = f32[32,3,4,32]{3,2,1,0:T(4,128)S(1)} all-gather(f32[1,3,4,32]{3,2,1,0:T(4,128)S(1)} %maximum_multiply_fusion), channel_id=1, replica_groups=mesh['task'=4,'mp'=8] {'task','mp'}, dimensions={0}, use_global_device_ids=true | all-gather | bytes 50688 | tf_op jit(solution)/shard_map/all_gather | solution.py:132
  300.7 0.1 select_reduce_fusion.3
  300.9 0.7 squeeze.17
  301.6 0.7 squeeze.16
  302.3 0.7 squeeze.15
  302.9 1.1 select_reduce_fusion
  (88 shorter events, 1.8 us)
Async XLA Ops:
  7.2 22.4 %copy-start = (bf16[1024,1024]{1,0:T(8,128)(2,1)S(1)}, bf16[1024,1024]{1,0:T(8,128)(2,1)}, u32[]{:S(2)}) copy-start(bf16[1024,1024]{1,0:T(8,128)(2,1)} %param.16) | copy-start | bytes 6291460
  7.2 33.5 %all-gather.5.cloned.1.call-start = ((), (), s32[]{:S(2)}) async-start(), calls=%async_computation.1 | async-start | bytes 2359296 | tf_op jit(solution)/shard_map/all_gather | solution.py:33
  9.2 89.9 %all-gather.7.cloned.1.call-start = ((), (), s32[]{:S(2)}) async-start(), calls=%async_computation.2 | async-start | bytes 2359296 | tf_op jit(solution)/shard_map/all_gather | solution.py:33
  29.6 2.6 copy-start.4
  35.1 1.2 copy-start.10
  40.7 4.9 %copy-start.5 = (bf16[256,4096]{1,0:T(8,128)(2,1)S(1)}, bf16[256,4096]{1,0:T(8,128)(2,1)}, u32[]{:S(2)}) copy-start(bf16[256,4096]{1,0:T(8,128)(2,1)} %all-gather.5.cloned.1.call-done) | copy-start | bytes 6291460
  50.4 18.0 %copy-start.2 = (f32[256,512]{1,0:T(8,128)S(1)}, f32[256,512]{1,0:T(8,128)}, u32[]{:S(2)}) copy-start(f32[256,512]{1,0:T(8,128)} %param.11) | copy-start | bytes 1572868
  50.4 20.7 %copy-start.3 = (bf16[256,1024]{0,1:T(8,128)(2,1)S(1)}, bf16[256,1024]{0,1:T(8,128)(2,1)}, u32[]{:S(2)}) copy-start(bf16[256,1024]{0,1:T(8,128)(2,1)} %get-tuple-element.50) | copy-start | bytes 1572868
  70.9 86.6 %all-gather.9.cloned.1.call-start = ((), (), s32[]{:S(2)}) async-start(), calls=%async_computation.3 | async-start | bytes 2359296 | tf_op jit(solution)/shard_map/all_gather | solution.py:33
  99.1 4.9 %copy-start.6 = (bf16[256,4096]{1,0:T(8,128)(2,1)S(1)}, bf16[256,4096]{1,0:T(8,128)(2,1)}, u32[]{:S(2)}) copy-start(bf16[256,4096]{1,0:T(8,128)(2,1)} %all-gather.7.cloned.1.call-done) | copy-start | bytes 6291460
  129.2 85.7 %all-gather.11.cloned.1.call-start = ((), (), s32[]{:S(2)}) async-start(), calls=%async_computation.4 | async-start | bytes 2359296 | tf_op jit(solution)/shard_map/all_gather | solution.py:33
  157.4 4.9 %copy-start.7 = (bf16[256,4096]{1,0:T(8,128)(2,1)S(1)}, bf16[256,4096]{1,0:T(8,128)(2,1)}, u32[]{:S(2)}) copy-start(bf16[256,4096]{1,0:T(8,128)(2,1)} %all-gather.9.cloned.1.call-done) | copy-start | bytes 6291460
  214.9 4.9 %copy-start.8 = (bf16[256,4096]{1,0:T(8,128)(2,1)S(1)}, bf16[256,4096]{1,0:T(8,128)(2,1)}, u32[]{:S(2)}) copy-start(bf16[256,4096]{1,0:T(8,128)(2,1)} %all-gather.11.cloned.1.call-done) | copy-start | bytes 6291460
  243.1 59.8 %all-to-all-start = ((bf16[4,256,512]{2,1,0:T(8,128)(2,1)}), bf16[4,256,512]{2,1,0:T(8,128)(2,1)S(1)}, u32[]{:S(2)}, u32[]{:S(2)}) async-start(bf16[4,256,512]{2,1,0:T(8,128)(2,1)} %select_convert_fusion), calls=%async_computation | async-start | bytes 2097152 | tf_op jit(solution)/shard_map/all_to_all | solution.py:106
  248.7 5.4 %copy-start.9 = (bf16[1024,2]{0,1:T(2,128)(2,1)S(1)}, bf16[1024,2]{0,1:T(2,128)(2,1)}, u32[]{:S(2)}) copy-start(bf16[1024,2]{0,1:T(2,128)(2,1)} %param.21) | copy-start | bytes 12292
  248.7 55.3 %copy-start.1 = (bf16[1024,1024]{1,0:T(8,128)(2,1)S(1)}, bf16[1024,1024]{1,0:T(8,128)(2,1)}, u32[]{:S(2)}) copy-start(bf16[1024,1024]{1,0:T(8,128)(2,1)} %param.16) | copy-start | bytes 6291460
Sparse Core Ops, SparseCore 0:
  9.9 30.8 all-gather.4
  71.0 28.0 all-gather.6
  129.3 28.0 all-gather.8
  186.8 28.0 all-gather.10
where the time goes:
time: 312 us; the launch traced here: 311 us
  blocking collectives  108 us (35%)
  waiting for transfers between devices  83 us (27%)
  matrix products  68.2 us (22%)
  other arithmetic  17.7 us (6%)
  local copies, waits for them, and re-layouts  14.2 us (5%)
  between operations  14.2 us (5%)
  starting transfers between devices  4.94 us (2%)
    all_gather x4, waiting for transfers between devices, recurrence(): gathered = lax.all_gather(low, 'mp', axis=1, tiled=True)  83 us
    dot_general x17, matrix products, product(): return jnp.dot(rows_in, weight, preferred_element_type=jnp.float32)  68.2 us
    psum x4, blocking collectives, recurrence(): sums, squares = lax.psum(jnp.stack([sums, squares]), 'mp')  52.6 us
    all_gather x1, blocking collectives, on_device(): spread = lax.all_gather(results, ('task', 'mp'))  40 us
    all_gather x1, blocking collectives, on_device(): packed = lax.all_gather(packed, 'task')  15.7 us
    convert_element_type x4, other arithmetic, recurrence(): low = carried.astype(jnp.bfloat16)  8.9 us
  transfers between devices with their start and end apart: 5, of which 4 were waited for; matrix products, arithmetic and copies ran while one was open for 10% of the time, Pallas kernels for 0%

commit v1 on v0

--- a/solution.py
+++ b/solution.py
@@ -36,7 +36,8 @@
         parts = [product(joined, gate_weight[part]) for part in range(3)]
         sums = sum((jnp.sum(part, axis=1) for part in parts))
         squares = sum((jnp.sum(part * part, axis=1) for part in parts))
-        sums, squares = lax.psum(jnp.stack([sums, squares]), "mp")
+        recover_loads_all = lambda field: lax.all_gather(field, axis_name="mp").sum(axis=0)
+        sums, squares = recover_loads_all(jnp.stack([sums, squares]))
         average = sums / (3 * det_full)
         inverse = lax.rsqrt(squares / (3 * det_full) - average * average + 1e-05)
         normed = [(part - average[:, None]) * inverse[:, None] for part in parts]

time: 312 us -> 296 us (0.949)
  blocking collectives: 108 us -> 93.1 us
    psum x4 -> x0, blocking collectives: 52.6 us -> none  [recurrence(): sums, squares = lax.psum(jnp.stack([sums, squares]), 'mp')]
    all_gather x0 -> x4, blocking collectives: none -> 35.7 us  [recurrence(): lax.all_gather(field, axis_name='mp').sum(axis=0)]
  transfers between devices with their start and end apart: 5 -> 5, of which waited for: 4 -> 4; matrix products, arithmetic and copies ran while one was open for 10% -> 11% of each run, Pallas kernels for 0% -> 0%
where the time goes in v1:
time: 296 us; the launch traced here: 295 us
  blocking collectives  93.1 us (31%)
  waiting for transfers between devices  83 us (28%)
  matrix products  68.2 us (23%)
  other arithmetic  17.8 us (6%)
  local copies, waits for them, and re-layouts  14.2 us (5%)
  between operations  14.2 us (5%)
  starting transfers between devices  4.94 us (2%)
    all_gather x4, waiting for transfers between devices, recurrence(): gathered = lax.all_gather(low, 'mp', axis=1, tiled=True)  82.9 us
    dot_general x17, matrix products, product(): return jnp.dot(rows_in, weight, preferred_element_type=jnp.float32)  68.2 us
    all_gather x1, blocking collectives, on_device(): spread = lax.all_gather(results, ('task', 'mp'))  41.7 us
    all_gather x4, blocking collectives, recurrence(): lax.all_gather(field, axis_name='mp').sum(axis=0)  35.7 us
    all_gather x1, blocking collectives, on_device(): packed = lax.all_gather(packed, 'task')  15.7 us
    convert_element_type x4, other arithmetic, recurrence(): low = carried.astype(jnp.bfloat16)  8.9 us
  transfers between devices with their start and end apart: 5, of which 4 were waited for; matrix products, arithmetic and copies ran while one was open for 11% of the time, Pallas kernels for 0%

profile of v1, /device:TPU:0, one launch (start us, length us, event | category | flops | bytes accessed | tf_op | source)
XLA Modules:
  0.0 295.4 jit_solution(3904869448127259675)
XLA Ops:
  7.2 1.9 convert_element_type.50
  9.2 0.7 convert_bitcast_fusion
  9.9 0.7 reduce_window_sum.11
  10.8 0.1 broadcast_in_dim.159
  11.0 0.9 convert.10
  12.0 15.7 %all_gather.44 = bf16[4,4,33,256]{3,1,2,0:T(4,128)(2,1)S(1)} all-gather(bf16[1,4,33,256]{3,1,2,0:T(4,128)(2,1)S(1)} %pad_maximum_fusion.16), channel_id=1, replica_groups=mesh['task'=4,'mp'=8] {'task'}, dimensions={0}, use_global_device_ids=true | all-gather | bytes 337920 | tf_op jit(solution)/shard_map/all_gather | solution.py:77
  27.7 0.2 select_reduce_fusion.1
  27.9 0.1 copy.59
  28.0 0.5 eq.155
  28.6 1.0 copy.69
  29.6 2.6 fusion
  32.2 1.5 fusion.47
  33.7 1.4 multiply_convert_fusion
  35.1 0.9 fusion.64
  36.0 0.2 copy.60
  36.3 0.1 select_reduce_fusion.4
  36.5 4.2 %all-gather.13.cloned.1.call-done = bf16[256,4096]{1,0:T(8,128)(2,1)} async-done(((bf16[256,512]{1,0:T(8,128)(2,1)}), bf16[256,4096]{1,0:T(8,128)(2,1)}) %all-gather.13.cloned.1.call-update) | async-done | bytes 2097168 | tf_op jit(solution)/shard_map/all_gather | solution.py:33
  40.7 4.9 %fusion.59 = (f32[256]{0:T(256)S(1)}, f32[256]{0:T(256)S(1)}, f32[256,512]{1,0:T(8,128)S(1)}) fusion(bf16[3,5120,512]{2,1,0:T(8,128)(2,1)} %bitcast.134, bf16[256,4096]{1,0:T(8,128)(2,1)} %all-gather.13.cloned.1.call-done, bf16[256,1024]{1,0:T(8,128)(2,1)S(1)} %copy.60), kind=kOutput, calls=%fused_computation.170 | convolution fusion | flops 1347812864 | bytes 8390656 | tf_op jit(solution)/shard_map/dot_general | solution.py:24
  45.6 4.8 %fusion.58 = (f32[256]{0:T(256)S(1)}, f32[256]{0:T(256)S(1)}, f32[256,512]{1,0:T(8,128)}) fusion(bf16[3,5120,512]{2,1,0:T(8,128)(2,1)} %bitcast.135, bf16[256,4096]{1,0:T(8,128)(2,1)S(1)} %copy-done.5, bf16[256,1024]{1,0:T(8,128)(2,1)S(1)} %copy.60), kind=kOutput, calls=%fused_computation.169 | convolution fusion | flops 1347812864 | bytes 8390656 | tf_op jit(solution)/shard_map/dot_general | solution.py:24
  50.4 4.9 %fusion.60 = (f32[256]{0:T(256)S(1)}, f32[256]{0:T(256)S(1)}, f32[256,512]{1,0:T(8,128)}) fusion(bf16[3,5120,512]{2,1,0:T(8,128)(2,1)} %bitcast.136, bf16[256,4096]{1,0:T(8,128)(2,1)S(1)} %copy-done.5, bf16[256,1024]{1,0:T(8,128)(2,1)S(1)} %copy.60), kind=kOutput, calls=%fused_computation.171 | convolution fusion | flops 1347812864 | bytes 8390656 | tf_op jit(solution)/shard_map/dot_general | solution.py:24
  55.4 8.9 %all-gather.4 = f32[8,2,256]{2,1,0:T(2,128)S(1)} all-gather(f32[1,2,256]{2,1,0:T(2,128)S(1)} %maximum_bitcast_fusion), channel_id=2, replica_groups=mesh['task'=4,'mp'=8] {'mp'}, dimensions={0}, use_global_device_ids=true | all-gather | bytes 18432 | tf_op jit(solution)/shard_map/all_gather | solution.py:39
  64.3 2.4 fusion.63
  66.7 0.2 all-gather.17.cloned.1.call-start
  66.9 0.2 copy.61
  67.1 27.8 %all-gather.15.cloned.1.call-done = bf16[256,4096]{1,0:T(8,128)(2,1)} async-done(((bf16[256,512]{1,0:T(8,128)(2,1)}), bf16[256,4096]{1,0:T(8,128)(2,1)}) %all-gather.15.cloned.1.call-update) | async-done | bytes 2097168 | tf_op jit(solution)/shard_map/all_gather | solution.py:33
  94.9 4.9 %fusion.56 = (f32[256]{0:T(256)S(1)}, f32[256]{0:T(256)S(1)}, f32[256,512]{1,0:T(8,128)S(1)}) fusion(bf16[3,5120,512]{2,1,0:T(8,128)(2,1)} %bitcast.137, bf16[256,4096]{1,0:T(8,128)(2,1)} %all-gather.15.cloned.1.call-done, bf16[256,1024]{1,0:T(8,128)(2,1)S(1)} %copy.61), kind=kOutput, calls=%fused_computation.167 | convolution fusion | flops 1347812864 | bytes 8390656 | tf_op jit(solution)/shard_map/dot_general | solution.py:24
  99.8 4.8 %fusion.55 = (f32[256]{0:T(256)S(1)}, f32[256]{0:T(256)S(1)}, f32[256,512]{1,0:T(8,128)}) fusion(bf16[3,5120,512]{2,1,0:T(8,128)(2,1)} %bitcast.138, bf16[256,4096]{1,0:T(8,128)(2,1)S(1)} %copy-done.6, bf16[256,1024]{1,0:T(8,128)(2,1)S(1)} %copy.61), kind=kOutput, calls=%fused_computation.166 | convolution fusion | flops 1347812864 | bytes 8390656 | tf_op jit(solution)/shard_map/dot_general | solution.py:24
  104.6 4.8 %fusion.57 = (f32[256]{0:T(256)S(1)}, f32[256]{0:T(256)S(1)}, f32[256,512]{1,0:T(8,128)}) fusion(bf16[3,5120,512]{2,1,0:T(8,128)(2,1)} %bitcast.139, bf16[256,4096]{1,0:T(8,128)(2,1)S(1)} %copy-done.6, bf16[256,1024]{1,0:T(8,128)(2,1)S(1)} %copy.61), kind=kOutput, calls=%fused_computation.168 | convolution fusion | flops 1347812864 | bytes 8390656 | tf_op jit(solution)/shard_map/dot_general | solution.py:24
  109.5 8.9 %all-gather.5 = f32[8,2,256]{2,1,0:T(2,128)S(1)} all-gather(f32[1,2,256]{2,1,0:T(2,128)S(1)} %maximum_bitcast_fusion.1), channel_id=3, replica_groups=mesh['task'=4,'mp'=8] {'mp'}, dimensions={0}, use_global_device_ids=true | all-gather | bytes 18432 | tf_op jit(solution)/shard_map/all_gather | solution.py:39
  118.4 2.4 fusion.62
  120.8 0.2 copy.62
  121.0 28.0 %all-gather.17.cloned.1.call-done = bf16[256,4096]{1,0:T(8,128)(2,1)} async-done(((bf16[256,512]{1,0:T(8,128)(2,1)}), bf16[256,4096]{1,0:T(8,128)(2,1)}) %all-gather.17.cloned.1.call-update) | async-done | bytes 2097168 | tf_op jit(solution)/shard_map/all_gather | solution.py:33
  149.0 4.9 %fusion.53 = (f32[256]{0:T(256)S(1)}, f32[256]{0:T(256)S(1)}, f32[256,512]{1,0:T(8,128)S(1)}) fusion(bf16[3,5120,512]{2,1,0:T(8,128)(2,1)} %bitcast.140, bf16[256,4096]{1,0:T(8,128)(2,1)} %all-gather.17.cloned.1.call-done, bf16[256,1024]{1,0:T(8,128)(2,1)S(1)} %copy.62), kind=kOutput, calls=%fused_computation.164 | convolution fusion | flops 1347812864 | bytes 8390656 | tf_op jit(solution)/shard_map/dot_general | solution.py:24
  153.9 4.1 %fusion.52 = (f32[256]{0:T(256)S(1)}, f32[256]{0:T(256)S(1)}, f32[256,512]{1,0:T(8,128)S(1)}) fusion(bf16[3,5120,512]{2,1,0:T(8,128)(2,1)} %bitcast.141, bf16[256,4096]{1,0:T(8,128)(2,1)S(1)} %copy-done.7, bf16[256,1024]{1,0:T(8,128)(2,1)S(1)} %copy.62), kind=kOutput, calls=%fused_computation.163 | convolution fusion | flops 1347812864 | bytes 8390656 | tf_op jit(solution)/shard_map/dot_general | solution.py:24
  158.1 4.8 %fusion.54 = (f32[256]{0:T(256)S(1)}, f32[256]{0:T(256)S(1)}, f32[256,512]{1,0:T(8,128)}) fusion(bf16[3,5120,512]{2,1,0:T(8,128)(2,1)} %bitcast.142, bf16[256,4096]{1,0:T(8,128)(2,1)S(1)} %copy-done.7, bf16[256,1024]{1,0:T(8,128)(2,1)S(1)} %copy.62), kind=kOutput, calls=%fused_computation.165 | convolution fusion | flops 1347812864 | bytes 8390656 | tf_op jit(solution)/shard_map/dot_general | solution.py:24
  162.9 8.9 %all-gather.6 = f32[8,2,256]{2,1,0:T(2,128)S(1)} all-gather(f32[1,2,256]{2,1,0:T(2,128)S(1)} %maximum_bitcast_fusion.2), channel_id=4, replica_groups=mesh['task'=4,'mp'=8] {'mp'}, dimensions={0}, use_global_device_ids=true | all-gather | bytes 18432 | tf_op jit(solution)/shard_map/all_gather | solution.py:39
  171.8 2.2 fusion.61
  174.1 0.1 copy.54
  174.7 0.1 eq.148
  174.8 0.2 copy.67
  175.1 1.0 constant_dynamic-slice_fusion.4
  176.0 1.7 constant_dynamic-slice_fusion.3
  177.7 1.7 constant_dynamic-slice_fusion.2
  179.4 22.9 %all-gather.19.cloned.1.call-done = bf16[256,4096]{1,0:T(8,128)(2,1)} async-done(((bf16[256,512]{1,0:T(8,128)(2,1)}), bf16[256,4096]{1,0:T(8,128)(2,1)}) %all-gather.19.cloned.1.call-update) | async-done | bytes 2097168 | tf_op jit(solution)/shard_map/all_gather | solution.py:33
  202.3 4.9 %fusion.49 = (f32[256]{0:T(256)S(1)}, f32[256]{0:T(256)S(1)}, f32[256,512]{1,0:T(8,128)S(1)}) fusion(bf16[3,5120,512]{2,1,0:T(8,128)(2,1)} %bitcast.143, bf16[256,4096]{1,0:T(8,128)(2,1)} %all-gather.19.cloned.1.call-done, bf16[256,1024]{1,0:T(8,128)(2,1)S(1)} %copy.67), kind=kOutput, calls=%fused_computation.160 | convolution fusion | flops 1347812864 | bytes 8390656 | tf_op jit(solution)/shard_map/dot_general | solution.py:24
  207.2 4.1 %fusion.48 = (f32[256]{0:T(256)S(1)}, f32[256]{0:T(256)S(1)}, f32[256,512]{1,0:T(8,128)S(1)}) fusion(bf16[3,5120,512]{2,1,0:T(8,128)(2,1)} %bitcast.144, bf16[256,4096]{1,0:T(8,128)(2,1)S(1)} %copy-done.8, bf16[256,1024]{1,0:T(8,128)(2,1)S(1)} %copy.67), kind=kOutput, calls=%fused_computation.159 | convolution fusion | flops 1347812864 | bytes 8390656 | tf_op jit(solution)/shard_map/dot_general | solution.py:24
  211.3 4.1 %fusion.50 = (f32[256]{0:T(256)S(1)}, f32[256]{0:T(256)S(1)}, f32[256,512]{1,0:T(8,128)S(1)}) fusion(bf16[3,5120,512]{2,1,0:T(8,128)(2,1)} %bitcast.145, bf16[256,4096]{1,0:T(8,128)(2,1)S(1)} %copy-done.8, bf16[256,1024]{1,0:T(8,128)(2,1)S(1)} %copy.67), kind=kOutput, calls=%fused_computation.161 | convolution fusion | flops 1347812864 | bytes 8390656 | tf_op jit(solution)/shard_map/dot_general | solution.py:24
  215.5 9.1 %all-gather.7 = f32[8,2,256]{2,1,0:T(2,128)S(1)} all-gather(f32[1,2,256]{2,1,0:T(2,128)S(1)} %maximum_bitcast_fusion.3), channel_id=5, replica_groups=mesh['task'=4,'mp'=8] {'mp'}, dimensions={0}, use_global_device_ids=true | all-gather | bytes 18432 | tf_op jit(solution)/shard_map/all_gather | solution.py:39
  224.6 0.5 add_select_fusion
  225.1 1.2 select_convert_fusion
  226.3 4.6 %all-to-all-start = ((bf16[4,256,512]{2,1,0:T(8,128)(2,1)}), bf16[4,256,512]{2,1,0:T(8,128)(2,1)S(1)}, u32[]{:S(2)}, u32[]{:S(2)}) async-start(bf16[4,256,512]{2,1,0:T(8,128)(2,1)} %select_convert_fusion), calls=%async_computation | async-start | bytes 2097152 | tf_op jit(solution)/shard_map/all_to_all | solution.py:107
  230.9 1.0 constant_dynamic-slice_fusion.1
  231.9 5.0 %fusion.51 = (f32[128]{0:T(128)S(1)}, f32[128]{0:T(128)S(1)}, f32[128,1024]{1,0:T(8,128)S(1)}) fusion(bf16[4096,1024]{1,0:T(8,128)(2,1)} %param.19, bf16[32,4096]{1,0:T(8,128)(2,1)S(1)} %constant_dynamic-slice_fusion.1, bf16[32,4096]{1,0:T(8,128)(2,1)} %constant_dynamic-slice_fusion.2, bf16[32,4096]{1,0:T(8,128)(2,1)} %constant_dynamic-slice_fusion.3, ...), kind=kOutput, calls=%fused_computation.162 | convolution fusion | flops 1078329088 | bytes 9962496 | tf_op jit(solution)/shard_map/dot_general | solution.py:24
  237.0 0.3 multiply_convert_fusion.1
  237.2 0.2 fusion.67
  237.6 2.9 fusion.17
  240.5 2.1 copy.63
  242.6 1.3 select_reduce_fusion.2
  244.0 41.7 %all_gather.55 = f32[32,3,4,32]{3,2,1,0:T(4,128)S(1)} all-gather(f32[1,3,4,32]{3,2,1,0:T(4,128)S(1)} %maximum_multiply_fusion), channel_id=1, replica_groups=mesh['task'=4,'mp'=8] {'task','mp'}, dimensions={0}, use_global_device_ids=true | all-gather | bytes 50688 | tf_op jit(solution)/shard_map/all_gather | solution.py:133
  285.6 0.1 select_reduce_fusion.3
  285.8 0.7 squeeze.17
  286.5 0.7 squeeze.16
  287.2 0.7 squeeze.15
  287.8 1.1 select_reduce_fusion
  (92 shorter events, 1.9 us)
Async XLA Ops:
  7.2 22.4 %copy-start = (bf16[1024,1024]{1,0:T(8,128)(2,1)S(1)}, bf16[1024,1024]{1,0:T(8,128)(2,1)}, u32[]{:S(2)}) copy-start(bf16[1024,1024]{1,0:T(8,128)(2,1)} %param.16) | copy-start | bytes 6291460
  7.2 33.5 %all-gather.13.cloned.1.call-start = ((), (), s32[]{:S(2)}) async-start(), calls=%async_computation.1 | async-start | bytes 2359296 | tf_op jit(solution)/shard_map/all_gather | solution.py:33
  9.2 85.7 %all-gather.15.cloned.1.call-start = ((), (), s32[]{:S(2)}) async-start(), calls=%async_computation.2 | async-start | bytes 2359296 | tf_op jit(solution)/shard_map/all_gather | solution.py:33
  29.6 2.6 copy-start.4
  35.1 1.2 copy-start.10
  40.7 4.9 %copy-start.5 = (bf16[256,4096]{1,0:T(8,128)(2,1)S(1)}, bf16[256,4096]{1,0:T(8,128)(2,1)}, u32[]{:S(2)}) copy-start(bf16[256,4096]{1,0:T(8,128)(2,1)} %all-gather.13.cloned.1.call-done) | copy-start | bytes 6291460
  50.4 13.8 %copy-start.2 = (f32[256,512]{1,0:T(8,128)S(1)}, f32[256,512]{1,0:T(8,128)}, u32[]{:S(2)}) copy-start(f32[256,512]{1,0:T(8,128)} %param.11) | copy-start | bytes 1572868
  50.4 16.5 %copy-start.3 = (bf16[256,1024]{0,1:T(8,128)(2,1)S(1)}, bf16[256,1024]{0,1:T(8,128)(2,1)}, u32[]{:S(2)}) copy-start(bf16[256,1024]{0,1:T(8,128)(2,1)} %get-tuple-element.50) | copy-start | bytes 1572868
  66.7 82.3 %all-gather.17.cloned.1.call-start = ((), (), s32[]{:S(2)}) async-start(), calls=%async_computation.3 | async-start | bytes 2359296 | tf_op jit(solution)/shard_map/all_gather | solution.py:33
  94.9 4.9 %copy-start.6 = (bf16[256,4096]{1,0:T(8,128)(2,1)S(1)}, bf16[256,4096]{1,0:T(8,128)(2,1)}, u32[]{:S(2)}) copy-start(bf16[256,4096]{1,0:T(8,128)(2,1)} %all-gather.15.cloned.1.call-done) | copy-start | bytes 6291460
  120.8 81.5 %all-gather.19.cloned.1.call-start = ((), (), s32[]{:S(2)}) async-start(), calls=%async_computation.4 | async-start | bytes 2359296 | tf_op jit(solution)/shard_map/all_gather | solution.py:33
  149.0 4.9 %copy-start.7 = (bf16[256,4096]{1,0:T(8,128)(2,1)S(1)}, bf16[256,4096]{1,0:T(8,128)(2,1)}, u32[]{:S(2)}) copy-start(bf16[256,4096]{1,0:T(8,128)(2,1)} %all-gather.17.cloned.1.call-done) | copy-start | bytes 6291460
  202.3 4.9 %copy-start.8 = (bf16[256,4096]{1,0:T(8,128)(2,1)S(1)}, bf16[256,4096]{1,0:T(8,128)(2,1)}, u32[]{:S(2)}) copy-start(bf16[256,4096]{1,0:T(8,128)(2,1)} %all-gather.19.cloned.1.call-done) | copy-start | bytes 6291460
  226.3 61.5 %all-to-all-start = ((bf16[4,256,512]{2,1,0:T(8,128)(2,1)}), bf16[4,256,512]{2,1,0:T(8,128)(2,1)S(1)}, u32[]{:S(2)}, u32[]{:S(2)}) async-start(bf16[4,256,512]{2,1,0:T(8,128)(2,1)} %select_convert_fusion), calls=%async_computation | async-start | bytes 2097152 | tf_op jit(solution)/shard_map/all_to_all | solution.py:107
  231.9 5.4 %copy-start.9 = (bf16[1024,2]{0,1:T(2,128)(2,1)S(1)}, bf16[1024,2]{0,1:T(2,128)(2,1)}, u32[]{:S(2)}) copy-start(bf16[1024,2]{0,1:T(2,128)(2,1)} %param.21) | copy-start | bytes 12292
  231.9 57.0 %copy-start.1 = (bf16[1024,1024]{1,0:T(8,128)(2,1)S(1)}, bf16[1024,1024]{1,0:T(8,128)(2,1)}, u32[]{:S(2)}) copy-start(bf16[1024,1024]{1,0:T(8,128)(2,1)} %param.16) | copy-start | bytes 6291460
Sparse Core Ops, SparseCore 0:
  9.9 30.8 all-gather.12
  66.8 28.0 all-gather.14
  120.9 28.0 all-gather.16
  174.2 28.0 all-gather.18
